TPU v7x, 32 devices: a whole 2x2x4 slice. The times are simulated.
32 devices in a mesh: seq: 4 (over y, x), tp: 4 (over z), grp: 2 (over core).
Axes of the slice: x: 2, y: 2, z: 4, core: 2. Of those that a mesh axis runs over, the one named last changes fastest.
Arguments:
- query: bfloat16 [16, 64, 8192], P('grp', None, 'tp'), parts along dimension 0, may hold values from -15 to 15
- cache: bfloat16 [16, 4096, 8, 256], P('grp', 'tp', 'seq'), parts along dimension 0, may hold values from -6 to 6
- head_of_slot: int32 [16], P('grp'), parts along dimension 0, may hold values from 0 to 7, each once
- lengths: int32 [16], P('grp'), parts along dimension 0, may hold values from 2048 to 4096
- out_weight: bfloat16 [8192, 8192], P('tp', 'seq'), may hold values from -0.0625 to 0.0625
Outputs:
- projected: bfloat16 [16, 64, 8192], P(('grp', 'tp'), None, 'seq'), parts along dimension 0
There are 2 independent parts, one for each index of `grp`. A program takes and returns all parts, laid end to end along the dimension named above; an argument that names none is the same for every part. Nothing has to cross between parts.
Inputs may be any that keep to these rules, and one draw needn't show every extreme that they name: head_of_slot names every KV head exactly once.
All inputs are finite; a program needn't handle non-finite values.
Results may differ from a plain program's by a relative error of at most 0.01.
Values may be sent and summed in bfloat16 or wider, within the bound.
A program may use at most 128 MiB of HBM per device.

v0:
```python
import functools
import math

import jax
import jax.numpy as jnp
from jax import lax
from jax.experimental import pallas as pl
from jax.experimental.pallas import tpu as pltpu
from jax.sharding import PartitionSpec as P

HQ = 64
KVH = 8
CHUNKS = 2
MASKED_SCORE = -1e30
FLOOR = -1e29
MESH = pl.DeviceIdType.MESH


def slot_table(head_of_slot):
    slot_total = head_of_slot.shape[0]
    slot_ids = jnp.arange(slot_total, dtype=jnp.int32)
    return jnp.sum(
        jnp.where(head_of_slot[None, :] == slot_ids[:, None], slot_ids[None, :], 0), axis=1
    )


def greet(axes):
    barrier = pltpu.get_barrier_semaphore()
    total = 0
    for axis in axes:
        n = lax.axis_size(axis)
        me = lax.axis_index(axis)
        for k in range(1, n):
            pl.semaphore_signal(
                barrier, inc=1, device_id={axis: lax.rem(me + k, n)}, device_id_type=MESH
            )
            total += 1
    pl.semaphore_wait(barrier, total)


def remote(src, dst, send_sem, recv_sem, axis, k):
    n = lax.axis_size(axis)
    target = lax.rem(lax.axis_index(axis) + k, n)
    return pltpu.make_async_remote_copy(
        src_ref=src,
        dst_ref=dst,
        send_sem=send_sem,
        recv_sem=recv_sem,
        device_id={axis: target},
        device_id_type=MESH,
    )


def back(axis, index):
    n = lax.axis_size(axis)
    return lax.rem(lax.axis_index(axis) + n - index, n)


def gather_attend_kernel(
    dims, hos, lens, q_ref, kv_hbm, att_ref,
    raw, kv_ref, kv_sem, zq, xs, xr, osend, orecv, lsend, lrecv, scores,
    zq_s, zq_r, xq_s, xq_r, o_s, o_r, l_s, l_r, own_sem,
):
    nc, bq, nsq, hl, ns, per_tp, Lb, hd, G, T = dims
    n_tp, n_seq = lax.axis_size("tp"), lax.axis_size("seq")
    me_t, me_s = lax.axis_index("tp"), lax.axis_index("seq")
    rows = G * T
    block = math.gcd(Lb, 256)
    scale = math.log2(math.e) / math.sqrt(hd)
    fetch = pltpu.make_async_copy(kv_hbm, raw, kv_sem)
    fetch.start()
    greet(("tp", "seq"))

    zsends = [
        [remote(q_ref.at[c], zq[c].at[k], zq_s.at[c, k], zq_r.at[c, k], "tp", k) for k in range(1, n_tp)]
        for c in range(nc)
    ]
    owns = [pltpu.make_async_copy(q_ref.at[c], zq[c].at[0], own_sem.at[c]) for c in range(nc)]
    for c in range(nc):
        for copy in zsends[c]:
            copy.start()
        owns[c].start()

    xsends = [
        [remote(xs.at[c, k], xr.at[c, k], xq_s.at[c, k], xq_r.at[c, k], "seq", k) for k in range(1, n_seq)]
        for c in range(nc)
    ]

    def spread(c):
        owns[c].wait()
        for copy in zsends[c]:
            copy.wait_recv()
        for k in list(range(1, n_seq)) + [0]:
            target = xr if k == 0 else xs
            column = lax.rem(me_s + k, n_seq)
            for j in range(ns):
                head = hos[column * ns + j]
                target[c, k, j] = zq[c][back("tp", head // hl), head % hl]
            if k:
                xsends[c][k - 1].start()

    osends = [
        [remote(osend.at[c, k], orecv.at[c, k], o_s.at[c, k], o_r.at[c, k], "tp", k) for k in range(1, n_tp)]
        for c in range(nc)
    ]
    lsends = [
        [remote(lsend.at[c, k], lrecv.at[c, k], l_s.at[c, k], l_r.at[c, k], "tp", k) for k in range(1, n_tp)]
        for c in range(nc)
    ]

    def attend_pair(c, k, pair):
        x, slot = pair // ns, pair % ns
        plane = lax.rem(me_t + k, n_tp)
        local_seq = plane * bq + x
        whole_seq = plane * per_tp + c * bq + x
        source = back("seq", local_seq // nsq)
        queries = xr[c, source, slot, local_seq % nsq].reshape(rows, hd)
        visible_end = lens[whole_seq] - me_t * Lb
        limits = visible_end - T + lax.broadcasted_iota(jnp.int32, (1, rows), 1) % T
        top = jnp.full((1, rows), FLOOR, jnp.float32)
        for i in range(Lb // block):
            s = lax.dot_general(
                kv_ref[slot, whole_seq, i * block : (i + 1) * block, :hd],
                queries,
                (((1,), (1,)), ((), ())),
                preferred_element_type=jnp.float32,
            )
            pos = i * block + lax.broadcasted_iota(jnp.int32, (block, 1), 0)
            s = jnp.where(pos <= limits, s * scale, MASKED_SCORE)
            scores[i * block : (i + 1) * block, :] = s
            top = jnp.maximum(top, jnp.max(s, axis=0, keepdims=True))
        total = jnp.zeros((1, rows), jnp.float32)
        out = jnp.zeros((hd, rows), jnp.float32)
        for i in range(Lb // block):
            w = jnp.exp2(scores[i * block : (i + 1) * block, :] - top)
            total = total + jnp.sum(w, axis=0, keepdims=True)
            out = out + lax.dot_general(
                kv_ref[slot, whole_seq, i * block : (i + 1) * block, hd:],
                w.astype(jnp.bfloat16),
                (((0,), (0,)), ((), ())),
                preferred_element_type=jnp.float32,
            )
        total = jnp.maximum(total, 1e-30)
        o_to, l_to = (orecv, lrecv) if k == 0 else (osend, lsend)
        o_to[c, k, x, slot] = (out / total).astype(jnp.bfloat16)
        l_to[c, k, x, slot] = top + jnp.log2(total)

    def attend(c):
        for copy in xsends[c]:
            copy.wait_recv()
        order = sorted(range(1, n_tp), key=lambda k: abs(k - n_tp / 2)) + [0]
        for k in order:
            lax.fori_loop(0, bq * ns, lambda pair, _: (attend_pair(c, k, pair), 0)[1], 0)
            if k:
                osends[c][k - 1].start()
                lsends[c][k - 1].start()

    def merge(c):
        for k in range(n_tp - 1):
            osends[c][k].wait_recv()
            lsends[c][k].wait_recv()

        def one(pair, _):
            x, slot = pair // ns, pair % ns
            ls = [lrecv[c, k, x, slot] for k in range(n_tp)]
            top = functools.reduce(jnp.maximum, ls)
            ws = [jnp.exp2(l - top) for l in ls]
            inverse = 1.0 / sum(ws)
            out = jnp.zeros((hd, rows), jnp.float32)
            for k in range(n_tp):
                out = out + (ws[k] * inverse) * orecv[c, k, x, slot].astype(jnp.float32)
            att_ref[c, x, slot] = out.astype(jnp.bfloat16)
            return 0

        lax.fori_loop(0, bq * ns, one, 0)

    fetch.wait()
    step = math.gcd(Lb, 128)
    turns = Lb // step

    def split(turn, _):
        at = pl.ds(pl.multiple_of(turn % turns * step, step), step)
        for slot in range(ns):
            kv_ref[slot, turn // turns, at, :] = raw[turn // turns, at, slot, :]
        return 0

    lax.fori_loop(0, raw.shape[0] * turns, split, 0)
    for c in range(nc):
        spread(c)
        if c:
            attend(c - 1)
    attend(nc - 1)
    for c in range(nc):
        merge(c)
    for c in range(nc):
        for copy in zsends[c] + xsends[c] + osends[c] + lsends[c]:
            copy.wait_send()


def gather_attend(qm, kv, head_of_slot, lengths, dims):
    nc, bq, nsq, hl, ns, per_tp, Lb, hd, G, T = dims
    n_tp, n_seq = lax.axis_size("tp"), lax.axis_size("seq")
    rows = G * T
    bf, f32 = jnp.bfloat16, jnp.float32
    dma = pltpu.SemaphoreType.DMA
    vmem = pl.BlockSpec(memory_space=pltpu.VMEM)
    smem = pl.BlockSpec(memory_space=pltpu.SMEM)
    return pl.pallas_call(
        functools.partial(gather_attend_kernel, dims),
        out_shape=jax.ShapeDtypeStruct((nc, bq, ns, hd, rows), bf),
        in_specs=[smem, smem, vmem, pl.BlockSpec(memory_space=pl.ANY)],
        out_specs=vmem,
        scratch_shapes=[
            pltpu.VMEM(kv.shape, bf),
            pltpu.VMEM((ns, kv.shape[0], Lb, 2 * hd), bf),
            dma(()),
            [pltpu.VMEM((n_tp, hl, nsq, G, T, hd), bf)] * nc,
            pltpu.VMEM((nc, n_seq, ns, nsq, G, T, hd), bf),
            pltpu.VMEM((nc, n_seq, ns, nsq, G, T, hd), bf),
            pltpu.VMEM((nc, n_tp, bq, ns, hd, rows), bf),
            pltpu.VMEM((nc, n_tp, bq, ns, hd, rows), bf),
            pltpu.VMEM((nc, n_tp, bq, ns, 1, rows), f32),
            pltpu.VMEM((nc, n_tp, bq, ns, 1, rows), f32),
            pltpu.VMEM((Lb, rows), f32),
            dma((nc, n_tp)), dma((nc, n_tp)), dma((nc, n_seq)), dma((nc, n_seq)),
            dma((nc, n_tp)), dma((nc, n_tp)), dma((nc, n_tp)), dma((nc, n_tp)), dma((nc,)),
        ],
        compiler_params=pltpu.CompilerParams(
            collective_id=0, has_side_effects=True, vmem_limit_bytes=56 * 2**20
        ),
    )(head_of_slot, lengths, qm, kv)


def project_kernel(
    dims, soh, att_ref, w_hbm, out_ref,
    w_ref, xr, zs, zr, ag, own, ps, pr,
    x_s, x_r, z_s, z_r, a_s, a_r, p_s, p_r, w_sem, own_sem,
):
    nc, bq, hl, ns, sub, part, T = dims
    n_tp, n_seq = lax.axis_size("tp"), lax.axis_size("seq")
    me_t, me_s = lax.axis_index("tp"), lax.axis_index("seq")
    width, columns = w_ref.shape
    few = bq * sub
    load = pltpu.make_async_copy(w_hbm, w_ref, w_sem)
    greet(("tp", "seq"))
    xsends = [
        [
            remote(att_ref.at[c, lax.rem(me_s + k, n_seq)], xr[c].at[k], x_s.at[c, k], x_r.at[c, k], "seq", k)
            for k in range(1, n_seq)
        ]
        for c in range(nc)
    ]
    owns = [pltpu.make_async_copy(att_ref.at[c, me_s], xr[c].at[0], own_sem.at[c]) for c in range(nc)]
    for c in range(nc):
        for copy in xsends[c]:
            copy.start()
        owns[c].start()
    load.start()
    zsends = [
        [remote(zs.at[c, k], zr.at[c, k], z_s.at[c, k], z_r.at[c, k], "tp", k) for k in range(1, n_tp)]
        for c in range(nc)
    ]
    asends = [
        [remote(zr.at[c], ag.at[c, k], a_s.at[c, k], a_r.at[c, k], "seq", k) for k in range(1, n_seq)]
        for c in range(nc)
    ]
    psends = [
        [remote(ps.at[c, k], pr.at[c, k], p_s.at[c, k], p_r.at[c, k], "tp", k) for k in range(1, n_tp)]
        for c in range(nc)
    ]
    for c in range(nc):
        owns[c].wait()
        for copy in xsends[c]:
            copy.wait_recv()
        for k in list(range(1, n_tp)) + [0]:
            target = zr if k == 0 else zs
            plane = lax.rem(me_t + k, n_tp)
            for j in range(hl):
                slot = soh[plane * hl + j]
                picked = xr[c][back("seq", slot // ns), slot % ns]
                target[c, k, :, j * part : (j + 1) * part] = picked
            if k:
                zsends[c][k - 1].start()
    for c in range(nc):
        for copy in zsends[c]:
            copy.wait_recv()
        for copy in asends[c]:
            copy.start()
    load.wait()
    tile = math.gcd(columns, 512)
    for c in range(nc):
        for copy in asends[c]:
            copy.wait_recv()
        pieces = []
        for k in range(n_tp):
            j = (n_tp - k) % n_tp
            for p in range(n_seq):
                pieces.append(zr[c, j] if p == 0 else ag[c, p, j])
        rows = jnp.concatenate(pieces, axis=0)

        def column_tile(i, _):
            at = pl.ds(pl.multiple_of(i * tile, tile), tile)
            product = jnp.dot(rows, w_ref[:, at], preferred_element_type=jnp.float32)
            span = n_seq * few
            own[c, :, at] = product[:span]
            for k in range(1, n_tp):
                ps[c, k, :, at] = product[k * span : (k + 1) * span].astype(jnp.bfloat16)
            return 0

        lax.fori_loop(0, columns // tile, column_tile, 0)
        for copy in psends[c]:
            copy.start()
    for c in range(nc):
        for copy in psends[c]:
            copy.wait_recv()
        for p in range(n_seq):
            column = lax.rem(me_s + n_seq - p, n_seq)
            for x in range(bq):
                at = p * few + x * sub
                total = own[c, at : at + sub]
                for k in range(1, n_tp):
                    total = total + pr[c, k, at : at + sub].astype(jnp.float32)
                out_ref[c * bq + x, pl.ds(pl.multiple_of(column * sub, sub), sub)] = total.astype(jnp.bfloat16)
    for c in range(nc):
        for copy in xsends[c] + zsends[c] + asends[c] + psends[c]:
            copy.wait_send()


def project(att, weight, slot_of_head, dims):
    nc, bq, hl, ns, sub, part, T = dims
    n_tp, n_seq = lax.axis_size("tp"), lax.axis_size("seq")
    width, columns = weight.shape
    few = bq * sub
    bf, f32 = jnp.bfloat16, jnp.float32
    dma = pltpu.SemaphoreType.DMA
    vmem = pl.BlockSpec(memory_space=pltpu.VMEM)
    return pl.pallas_call(
        functools.partial(project_kernel, dims),
        out_shape=jax.ShapeDtypeStruct((nc * bq, T, columns), bf),
        in_specs=[
            pl.BlockSpec(memory_space=pltpu.SMEM), vmem, pl.BlockSpec(memory_space=pl.ANY)
        ],
        out_specs=vmem,
        scratch_shapes=[
            pltpu.VMEM((width, columns), bf),
            [pltpu.VMEM((n_seq, ns, few, part), bf)] * nc,
            pltpu.VMEM((nc, n_tp, few, width), bf),
            pltpu.VMEM((nc, n_tp, few, width), bf),
            pltpu.VMEM((nc, n_seq, n_tp, few, width), bf),
            pltpu.VMEM((nc, n_seq * few, columns), f32),
            pltpu.VMEM((nc, n_tp, n_seq * few, columns), bf),
            pltpu.VMEM((nc, n_tp, n_seq * few, columns), bf),
            dma((nc, n_seq)), dma((nc, n_seq)), dma((nc, n_tp)), dma((nc, n_tp)),
            dma((nc, n_seq)), dma((nc, n_seq)), dma((nc, n_tp)), dma((nc, n_tp)),
            dma(()), dma((nc,)),
        ],
        compiler_params=pltpu.CompilerParams(
            collective_id=1, has_side_effects=True, vmem_limit_bytes=48 * 2**20
        ),
    )(slot_of_head, att, weight)


def local(query, cache, head_of_slot, lengths, out_weight):
    G = HQ // KVH
    n_seq, n_tp = lax.axis_size("seq"), lax.axis_size("tp")
    me_s = lax.axis_index("seq")
    slot_of_head = slot_table(head_of_slot)
    B, T, width = query.shape
    Lb, ns, hd2 = cache.shape[1:]
    hd = hd2 // 2
    hl = KVH // n_tp
    per_tp = B // n_tp
    nc = math.gcd(CHUNKS, per_tp)
    bq = per_tp // nc
    nsq = n_tp * bq // n_seq
    sub = T // n_seq

    chunked = query.reshape(n_tp, nc, bq, T, width).transpose(1, 0, 2, 3, 4)
    chunked = chunked.reshape(nc, n_seq, nsq, T, width)
    mine = lax.dynamic_index_in_dim(chunked, me_s, 1, False)
    qm = mine.reshape(nc, nsq, T, hl, G, hd).transpose(0, 3, 1, 4, 2, 5)
    kv = cache
    att = gather_attend(
        qm, kv, head_of_slot, lengths, (nc, bq, nsq, hl, ns, per_tp, Lb, hd, G, T)
    )
    att = att.reshape(nc, bq, ns, hd, G, n_seq, sub).transpose(0, 5, 2, 1, 6, 4, 3)
    att = att.reshape(nc, n_seq, ns, bq * sub, G * hd)
    return project(att, out_weight, slot_of_head, (nc, bq, hl, ns, sub, G * hd, T))


def solution(mesh):
    in_specs = (
        P("grp", None, "tp"),
        P("grp", "tp", "seq", None),
        P("grp"),
        P("grp"),
        P("tp", "seq"),
    )
    out_specs = P(("grp", "tp"), None, "seq")
    return jax.shard_map(local, mesh=mesh, in_specs=in_specs, out_specs=out_specs, check_vma=False)
```

profile of v0, /device:TPU:0, one launch (start us, length us, event | category | flops | bytes accessed | tf_op | source)
XLA Modules:
  0.0 172.4 jit_solution(11986243077703983417)
XLA Ops:
  0.0 0.0 copy-start
  0.0 1.6 copy-done
  1.6 0.8 select_reduce_fusion.soh
  2.4 0.1 copy.15
  2.5 0.9 copy.17
  3.5 95.8 %shard_map.55 = bf16[2,1,2,128,512]{4,3,2,1,0:T(8,128)(2,1)} custom-call(s32[8]{0:T(128)} %hos.1, s32[8]{0:T(128)} %lens.1, bf16[2,2,1,8,64,128]{5,4,3,2,1,0:T(8,128)(2,1)} %bitcast.21, bf16[8,1024,2,256]{3,2,1,0:T(2,128)(2,1)} %kv_hbm.1), custom_call_target="tpu_custom_call" | custom-call | tf_op jit(solution)/shard_map/pallas_call | solution.py:208
  99.2 1.3 copy.13
  100.5 0.3 copy.14
  100.9 0.2 reshape.19.att_ref
  101.1 70.4 %shard_map.56 = bf16[2,64,2048]{2,1,0:T(8,128)(2,1)S(1)} custom-call(s32[8]{0:T(128)S(1)} %select_reduce_fusion.soh, bf16[2,4,2,16,1024]{4,3,2,1,0:T(8,128)(2,1)S(1)} %reshape.19.att_ref, bf16[2048,2048]{1,0:T(8,128)(2,1)} %w_hbm.1), custom_call_target="tpu_custom_call" | custom-call | tf_op jit(solution)/shard_map/pallas_call | solution.py:337
  171.6 0.8 copy.19
  (1 shorter events, 0.0 us)
Async XLA Ops:
  0.0 1.6 copy-start
where the time goes:
time: 174 us; the launch traced here: 172 us
  Pallas kernels  166 us (95%)
  local copies, waits for them, and re-layouts  5.35 us (3%)
    pallas_call x1, Pallas kernels, gather_attend(): pl.pallas_call(functools.partial(gather_attend_kernel, dims), out_shape=j...  95.8 us
    pallas_call x1, Pallas kernels, project(): pl.pallas_call(functools.partial(project_kernel, dims), out_shape=jax.Sha...  70.4 us

commit v1 on v0

--- a/solution.py
+++ b/solution.py
@@ -11,6 +11,10 @@
 HQ = 64
 KVH = 8
 CHUNKS = 2
+TOKEN_CUTS = 2
+PERIOD = 2.0
+AFTER = (0.0, 0.4, 0.8, 2.4, 3.9, 5.2, 6.2, 7.3, 8.7, 9.5)
+SPLIT_AT = (-0.1, 0.05, 0.3, 0.5, 1.6, 1.7, 3.3, 3.4)
 MASKED_SCORE = -1e30
 FLOOR = -1e29
 MESH = pl.DeviceIdType.MESH
@@ -360,6 +364,398 @@
     )(slot_of_head, att, weight)
 
 
+def line_kernel(
+    dims, hos, lens, q_hbm, kv_hbm, w_hbm, out_ref,
+    raw, kv_ref, w_ref, az, xs, xr, osend, orecv, lsend, lrecv, scores,
+    bs, bls, bm, blm, br, blr, xg, own, ds, dm, dr,
+    kv_sem, w_sem, q_sem,
+    a_s, a_r, xq_s, xq_r, o_s, o_r, l_s, l_r,
+    b_s, b_r, bl_s, bl_r, g_s, g_r, d_s, d_r,
+):
+    nth, tt, hl, ns, Lb, hd, G = dims
+    n_tp, n_seq = lax.axis_size("tp"), lax.axis_size("seq")
+    me_t, me_s = lax.axis_index("tp"), lax.axis_index("seq")
+    per_tp = out_ref.shape[0]
+    nc = per_tp * nth
+    T = nth * tt
+    rows = G * tt
+    columns = w_ref.shape[1]
+    half = me_t // 2
+    partner = me_t + 1 - 2 * (me_t % 2)
+    far_inner = 2 - half
+    far_outer = 3 - 3 * half
+    inner = me_t == 1 + half
+    outer = me_t == 3 * half
+    block = math.gcd(Lb, 256)
+    scale = math.log2(math.e) / math.sqrt(hd)
+    bf, f32 = jnp.bfloat16, jnp.float32
+
+    def part(c):
+        return c // nth, c % nth
+
+    def to(axis, target, src, dst, send, recv):
+        return pltpu.make_async_remote_copy(
+            src_ref=src, dst_ref=dst, send_sem=send, recv_sem=recv,
+            device_id={axis: target}, device_id_type=MESH,
+        )
+
+    def ring(target_of):
+        return [[target_of(c, k) for k in range(1, n_seq)] for c in range(nc)]
+
+    def block_to(c, i, plane, target):
+        return to("tp", target, az[c].at[plane], az[c].at[plane], a_s.at[c, i], a_r.at[c, i])
+
+    own_p = [block_to(c, 0, me_t, partner) for c in range(nc)]
+    own_f = [block_to(c, 1, me_t, far_inner) for c in range(nc)]
+    via_f = [block_to(c, 2, partner, far_inner) for c in range(nc)]
+    via_a = [block_to(c, 3, far_inner, partner) for c in range(nc)]
+    via_b = [block_to(c, 4, far_outer, partner) for c in range(nc)]
+    column = lambda k: lax.rem(me_s + k, n_seq)
+    xsends = ring(lambda c, k: to("seq", column(k), xs.at[c, k], xr.at[c, k], xq_s.at[c, k], xq_r.at[c, k]))
+    osends = ring(lambda c, k: to("seq", column(k), osend.at[c, k], orecv[c].at[k], o_s.at[c, k], o_r.at[c, k]))
+    lsends = ring(lambda c, k: to("seq", column(k), lsend.at[c, k], lrecv[c].at[k], l_s.at[c, k], l_r.at[c, k]))
+    gsends = ring(lambda c, k: to("seq", column(k), xg.at[c, 0], xg.at[c, k], g_s.at[c, k], g_r.at[c, k]))
+
+    def swap(c, send, mid, out, s, r):
+        return dict(
+            pair=to("tp", partner, send.at[c, 0], out.at[c, 0], s.at[c, 0], r.at[c, 0]),
+            lift=[to("tp", partner, send.at[c, i], mid.at[c, i - 1], s.at[c, i], r.at[c, i]) for i in (1, 2)],
+            cross=[
+                to("tp", target, send.at[c, i], out.at[c, 1], s.at[c, 2 + i], r.at[c, 3])
+                for i, target in ((1, far_inner), (2, far_outer))
+            ],
+        )
+
+    bz = [(swap(c, bs, bm, br, b_s, b_r), swap(c, bls, blm, blr, bl_s, bl_r)) for c in range(nc)]
+    dz = [(swap(c, ds, dm, dr, d_s, d_r),) for c in range(nc)]
+
+    def own_blocks(c):
+        x, th = part(c)
+        for j in range(hl):
+            for g in range(G):
+                yield pltpu.make_async_copy(
+                    q_hbm.at[me_s * per_tp + x, pl.ds(th * tt, tt), pl.ds((j * G + g) * hd, hd)],
+                    az[c].at[me_t, j, g],
+                    q_sem.at[c],
+                )
+
+    def ask_own(c):
+        pltpu.make_async_copy(az[c].at[me_t], az[c].at[me_t], q_sem.at[c]).wait()
+        own_p[c].start()
+
+        @pl.when(inner)
+        def _():
+            own_f[c].start()
+
+    def relay_a(c):
+        @pl.when(inner)
+        def _():
+            own_p[c].wait_recv()
+            via_f[c].start()
+            own_f[c].wait_recv()
+            via_a[c].start()
+
+    def relay_b(c):
+        @pl.when(inner)
+        def _():
+            via_f[c].wait_recv()
+            via_b[c].start()
+
+    def spread(c):
+        @pl.when(outer)
+        def _():
+            own_p[c].wait_recv()
+            via_a[c].wait_recv()
+            via_b[c].wait_recv()
+
+        for k in list(range(1, n_seq)) + [0]:
+            target = xr if k == 0 else xs
+            for j in range(ns):
+                head = hos[column(k) * ns + j]
+                target[c, k, j] = az[c][head // hl, head % hl]
+            if k:
+                xsends[c][k - 1].start()
+
+    def attend_pair(c, k, slot):
+        x, th = part(c)
+        seq = column(k) * per_tp + x
+        queries = xr[c, (n_seq - k) % n_seq, slot].reshape(rows, hd)
+        visible_end = lens[seq] - me_t * Lb
+        limits = visible_end - T + th * tt + lax.broadcasted_iota(jnp.int32, (1, rows), 1) % tt
+        top = jnp.full((1, rows), FLOOR, f32)
+        for i in range(Lb // block):
+            s = lax.dot_general(
+                kv_ref[slot, seq, i * block : (i + 1) * block, :hd],
+                queries,
+                (((1,), (1,)), ((), ())),
+                preferred_element_type=f32,
+            )
+            pos = i * block + lax.broadcasted_iota(jnp.int32, (block, 1), 0)
+            s = jnp.where(pos <= limits, s * scale, MASKED_SCORE)
+            scores[i * block : (i + 1) * block, :] = s
+            top = jnp.maximum(top, jnp.max(s, axis=0, keepdims=True))
+        total = jnp.zeros((1, rows), f32)
+        out = jnp.zeros((hd, rows), f32)
+        for i in range(Lb // block):
+            w = jnp.exp2(scores[i * block : (i + 1) * block, :] - top)
+            total = total + jnp.sum(w, axis=0, keepdims=True)
+            out = out + lax.dot_general(
+                kv_ref[slot, seq, i * block : (i + 1) * block, hd:],
+                w.astype(bf),
+                (((0,), (0,)), ((), ())),
+                preferred_element_type=f32,
+            )
+        total = jnp.maximum(total, 1e-30)
+        o_to = orecv[c].at[0] if k == 0 else osend.at[c, k]
+        l_to = lrecv[c].at[0] if k == 0 else lsend.at[c, k]
+        o_to[slot] = (out / total).astype(bf)
+        l_to[slot] = top + jnp.log2(total)
+
+    def attend(c):
+        for copy in xsends[c]:
+            copy.wait_recv()
+        for k in list(range(1, n_seq)) + [0]:
+            lax.fori_loop(0, ns, lambda slot, _: (attend_pair(c, k, slot), 0)[1], 0)
+            if k:
+                osends[c][k - 1].start()
+                lsends[c][k - 1].start()
+
+    def picked(c, plane, j):
+        head = plane * hl + j
+        slot = jnp.int32(0)
+        for s in range(n_seq * ns):
+            slot = jnp.maximum(slot, jnp.where(hos[s] == head, s, 0))
+        k = lax.rem(me_s + n_seq - slot // ns, n_seq)
+        return orecv[c][k, slot % ns], lrecv[c][k, slot % ns]
+
+    def merged(parts):
+        top = functools.reduce(jnp.maximum, [l for _, l in parts])
+        ws = [jnp.exp2(l - top) for _, l in parts]
+        total = functools.reduce(jnp.add, ws)
+        inverse = 1.0 / total
+        out = functools.reduce(
+            jnp.add, [(w * inverse) * o.astype(f32) for w, (o, _) in zip(ws, parts)]
+        )
+        return out, top + jnp.log2(total)
+
+    def put(c, i, plane):
+        for j in range(hl):
+            o, l = picked(c, plane, j)
+            bs[c, i, j] = o
+            bls[c, i, j] = l
+
+    def part_send(c):
+        for copy in osends[c] + lsends[c]:
+            copy.wait_recv()
+
+        @pl.when(outer)
+        def _():
+            for i, plane in ((1, far_inner), (2, far_outer)):
+                put(c, i, plane)
+                for z in bz[c]:
+                    z["lift"][i - 1].start()
+
+        put(c, 0, partner)
+        for z in bz[c]:
+            z["pair"].start()
+
+    def part_join(c):
+        @pl.when(inner)
+        def _():
+            for i, plane in ((2, far_outer), (1, far_inner)):
+                for z in bz[c]:
+                    z["lift"][i - 1].wait_recv()
+                for j in range(hl):
+                    o, l = merged([picked(c, plane, j), (bm[c, i - 1, j], blm[c, i - 1, j])])
+                    bs[c, i, j] = o.astype(bf)
+                    bls[c, i, j] = l
+                for z in bz[c]:
+                    z["cross"][i - 1].start()
+
+    def part_end(c):
+        for z in bz[c]:
+            z["pair"].wait_recv()
+            z["cross"][0].wait_recv()
+        for j in range(hl):
+            o, _ = merged([picked(c, me_t, j)] + [(br[c, i, j], blr[c, i, j]) for i in range(2)])
+            turned = o.T.astype(bf)
+            for g in range(G):
+                at = (j * G + g) * hd
+                xg[c, 0, :, at : at + hd] = turned[g * tt : (g + 1) * tt]
+        for copy in gsends[c]:
+            copy.start()
+
+    tile = math.gcd(columns, 512)
+
+    def project(c):
+        for copy in gsends[c]:
+            copy.wait_recv()
+        planes = [me_t, partner, far_inner, far_outer]
+        lhs = jnp.concatenate(
+            [xg[c, lax.rem(me_s + n_seq - p, n_seq)] for p in planes], axis=0
+        )
+
+        def column_tile(i, _):
+            at = pl.ds(pl.multiple_of(i * tile, tile), tile)
+            product = jnp.dot(lhs, w_ref[:, at], preferred_element_type=f32)
+            own[c, :, at] = product[:tt]
+            for i in range(3):
+                ds[c, i, :, at] = product[(i + 1) * tt : (i + 2) * tt].astype(bf)
+            return 0
+
+        lax.fori_loop(0, columns // tile, column_tile, 0)
+
+        @pl.when(outer)
+        def _():
+            for copy in dz[c][0]["lift"]:
+                copy.start()
+
+        dz[c][0]["pair"].start()
+
+    def sum_join(c):
+        z = dz[c][0]
+
+        @pl.when(inner)
+        def _():
+            for i in (2, 1):
+                z["lift"][i - 1].wait_recv()
+                ds[c, i] = (ds[c, i].astype(f32) + dm[c, i - 1].astype(f32)).astype(bf)
+                z["cross"][i - 1].start()
+
+    def sum_end(c):
+        x, th = part(c)
+        z = dz[c][0]
+        z["pair"].wait_recv()
+        z["cross"][0].wait_recv()
+        total = own[c] + dr[c, 0].astype(f32) + dr[c, 1].astype(f32)
+        out_ref[x, th * tt : (th + 1) * tt] = total.astype(bf)
+
+    step = math.gcd(Lb, 128)
+    turns = Lb // step
+    n_b = raw.shape[0]
+    seq_order = [p * per_tp + x for x in range(per_tp) for p in range(n_tp)]
+    fetches = [pltpu.make_async_copy(kv_hbm.at[b], raw.at[b], kv_sem.at[b]) for b in range(n_b)]
+
+    def split(index):
+        b = seq_order[index]
+        fetches[b].wait()
+
+        def turn(i, _):
+            at = pl.ds(pl.multiple_of(i * step, step), step)
+            for slot in range(ns):
+                kv_ref[slot, b, at, :] = raw[b, at, slot, :]
+            return 0
+
+        lax.fori_loop(0, turns, turn, 0)
+
+    load = pltpu.make_async_copy(w_hbm, w_ref, w_sem)
+
+    for c in range(nc):
+        for copy in own_blocks(c):
+            copy.start()
+    for b in seq_order:
+        fetches[b].start()
+    load.start()
+    greet(("tp", "seq"))
+
+    run = dict(
+        q=ask_own, ra=relay_a, rb=relay_b, sp=spread, at=attend, bs=part_send, bj=part_join,
+        be=part_end, pr=project, dj=sum_join, de=sum_end, kv=split, w=lambda _: load.wait(),
+    )
+    for name, c in order_of(nc, n_b):
+        run[name](c)
+
+    for c in range(nc):
+        own_p[c].wait_send()
+        for copy in xsends[c] + osends[c] + lsends[c] + gsends[c]:
+            copy.wait_send()
+        for z in bz[c] + dz[c]:
+            z["pair"].wait_send()
+
+        @pl.when(outer)
+        def _():
+            for z in bz[c] + dz[c]:
+                for copy in z["lift"]:
+                    copy.wait_send()
+
+        @pl.when(inner)
+        def _():
+            for copy in (own_f[c], via_f[c], via_a[c], via_b[c]):
+                copy.wait_send()
+            for z in bz[c] + dz[c]:
+                for copy in z["cross"]:
+                    copy.wait_send()
+
+
+def order_of(nc, n_b):
+    steps = ["ra", "rb", "sp", "at", "bs", "bj", "be", "pr", "dj", "de"]
+    after = dict(zip(steps, AFTER))
+    plan = []
+    for c in range(nc):
+        for place, name in enumerate(steps):
+            plan.append((c * PERIOD + after[name], place, name, c))
+        if c:
+            plan.append(((c - 1) * PERIOD + after["ra"] + 0.1, 0, "q", c))
+    for i in range(n_b):
+        plan.append((SPLIT_AT[i * len(SPLIT_AT) // n_b], 0, "kv", i))
+    plan.append((after["pr"] - 0.01, 0, "w", 0))
+    return [("q", 0)] + [(name, c) for _, _, name, c in sorted(plan, key=lambda e: (e[0], -e[1]))]
+
+
+def line_call(query, cache, head_of_slot, lengths, out_weight, nth):
+    n_seq, n_tp = lax.axis_size("seq"), lax.axis_size("tp")
+    G = HQ // KVH
+    B, T, _ = query.shape
+    Lb, ns, hd2 = cache.shape[1:]
+    hd = hd2 // 2
+    hl = KVH // n_tp
+    per_tp = B // n_tp
+    tt = T // nth
+    nc = per_tp * nth
+    rows = G * tt
+    columns = out_weight.shape[1]
+    bf, f32 = jnp.bfloat16, jnp.float32
+    dma = pltpu.SemaphoreType.DMA
+    v = pltpu.VMEM
+    anywhere = pl.BlockSpec(memory_space=pl.ANY)
+    smem = pl.BlockSpec(memory_space=pltpu.SMEM)
+    return pl.pallas_call(
+        functools.partial(line_kernel, (nth, tt, hl, ns, Lb, hd, G)),
+        out_shape=jax.ShapeDtypeStruct((per_tp, T, columns), bf),
+        in_specs=[smem, smem, anywhere, anywhere, anywhere],
+        out_specs=pl.BlockSpec(memory_space=pltpu.VMEM),
+        scratch_shapes=[
+            v(cache.shape, bf),
+            v((ns, B, Lb, 2 * hd), bf),
+            v(out_weight.shape, bf),
+            [v((n_tp, hl, G, tt, hd), bf)] * nc,
+            v((nc, n_seq, ns, G, tt, hd), bf),
+            v((nc, n_seq, ns, G, tt, hd), bf),
+            v((nc, n_seq, ns, hd, rows), bf),
+            [v((n_seq, ns, hd, rows), bf)] * nc,
+            v((nc, n_seq, ns, 1, rows), f32),
+            [v((n_seq, ns, 1, rows), f32)] * nc,
+            v((Lb, rows), f32),
+            v((nc, 3, hl, hd, rows), bf), v((nc, 3, hl, 1, rows), f32),
+            v((nc, 2, hl, hd, rows), bf), v((nc, 2, hl, 1, rows), f32),
+            v((nc, 2, hl, hd, rows), bf), v((nc, 2, hl, 1, rows), f32),
+            v((nc, n_seq, tt, hl * G * hd), bf),
+            v((nc, tt, columns), f32),
+            v((nc, 3, tt, columns), bf), v((nc, 2, tt, columns), bf), v((nc, 2, tt, columns), bf),
+            dma((B,)), dma(()), dma((nc,)),
+            dma((nc, 5)), dma((nc, 5)),
+            dma((nc, n_seq)), dma((nc, n_seq)),
+            dma((nc, n_seq)), dma((nc, n_seq)), dma((nc, n_seq)), dma((nc, n_seq)),
+            dma((nc, 5)), dma((nc, 4)), dma((nc, 5)), dma((nc, 4)),
+            dma((nc, n_seq)), dma((nc, n_seq)),
+            dma((nc, 5)), dma((nc, 4)),
+        ],
+        compiler_params=pltpu.CompilerParams(
+            collective_id=2, has_side_effects=True, vmem_limit_bytes=60 * 2**20
+        ),
+    )(head_of_slot, lengths, query, cache, out_weight)
+
+
 def local(query, cache, head_of_slot, lengths, out_weight):
     G = HQ // KVH
     n_seq, n_tp = lax.axis_size("seq"), lax.axis_size("tp")
@@ -370,6 +766,9 @@
     hd = hd2 // 2
     hl = KVH // n_tp
     per_tp = B // n_tp
+    nth = math.gcd(TOKEN_CUTS, T)
+    if n_tp == n_seq == 4 and HQ * hd == n_tp * width and T // nth % 16 == 0:
+        return line_call(query, cache, head_of_slot, lengths, out_weight, nth)
     nc = math.gcd(CHUNKS, per_tp)
     bq = per_tp // nc
     nsq = n_tp * bq // n_seq

time: 174 us -> 130 us (0.75); the launches traced: 172 us -> 130 us
  Pallas kernels: 166 us -> 128 us
  local copies, waits for them, and re-layouts: 5.35 us -> 1.88 us
    pallas_call x2 -> x1, Pallas kernels: 166 us -> 128 us  [line_call(): pl.pallas_call(functools.partial(line_kernel, (nth, tt, hl, ns, Lb, hd, G...]
where the time goes in v1:
time: 130 us
  Pallas kernels  128 us (98%)
  local copies, waits for them, and re-layouts  1.88 us (1%)
    pallas_call x1, Pallas kernels, line_call(): pl.pallas_call(functools.partial(line_kernel, (nth, tt, hl, ns, Lb, hd, G...  128 us

profile of v1, /device:TPU:0, one launch (start us, length us, event | category | flops | bytes accessed | tf_op | source)
XLA Modules:
  0.0 130.1 jit_solution(18044583395664414038)
XLA Ops:
  0.0 128.2 %shard_map.55 = bf16[2,64,2048]{2,1,0:T(8,128)(2,1)} custom-call(s32[8]{0:T(128)} %hos.1, s32[8]{0:T(128)} %lens.1, bf16[8,64,2048]{2,1,0:T(8,128)(2,1)} %q_hbm.1, bf16[8,1024,2,256]{3,2,1,0:T(2,128)(2,1)} %kv_hbm.1, bf16[2048,2048]{1,0:T(8,128)(2,1)} %w_hbm.1), custom_call_target="tpu_custom_call" | custom-call | tf_op jit(solution)/shard_map/pallas_call | solution.py:722
  128.2 1.9 %copy.7 = bf16[2,64,2048]{2,1,0:T(8,128)(2,1)} copy(bf16[2,64,2048]{2,1,0:T(8,128)(2,1)} %shard_map.55) | data formatting | bytes 1048576

commit v2 on v1

--- a/solution.py
+++ b/solution.py
@@ -11,10 +11,19 @@
 HQ = 64
 KVH = 8
 CHUNKS = 2
-TOKEN_CUTS = 2
-PERIOD = 2.0
-AFTER = (0.0, 0.4, 0.8, 2.4, 3.9, 5.2, 6.2, 7.3, 8.7, 9.5)
-SPLIT_AT = (-0.1, 0.05, 0.3, 0.5, 1.6, 1.7, 3.3, 3.4)
+CUTS = ((16, 32, 16), (16, 32, 16))
+ORDER = (
+    "q.0", "q.1", "kv.0", "ra.0", "kv.1", "ra.1", "kv.2", "rb.0", "kv.3", "rb.1", "q.5", "q.2",
+    "kv.4", "sp.0", "q.4", "a0.0", "sp.1", "a0.1", "ra.2", "a1.0", "a2.0", "ra.4", "kv.5", "a1.1",
+    "rb.2", "a3.0", "a2.1", "q.3", "rb.4", "ra.5", "sp.2", "a3.1", "bs.0", "kv.6", "sp.4", "bj.0",
+    "a0.2", "ra.3", "kv.7", "rb.5", "bs.1", "a0.4", "a1.2", "a2.2", "a3.2", "be.0", "bj.1",
+    "a1.4", "rb.3", "a2.4", "bs.2", "a3.4", "pr.0", "be.1", "sp.5", "bj.2", "sp.3", "a0.3",
+    "bs.4", "dj.0", "pr.1", "a0.5", "a1.5", "a2.5", "bj.4", "a1.3", "a2.3", "a3.5", "a3.3",
+    "dj.1", "bs.5", "be.2", "bs.3", "be.4", "pr.2", "bj.3", "bj.5", "pr.4", "dj.2", "be.3",
+    "be.5", "dj.4", "de.1", "pr.3", "de.0", "pr.5", "dj.3", "de.4", "de.2", "dj.5", "de.3",
+    "de.5",
+)
+FIRST_PROJECT = next(e for e in ORDER if e[:2] == "pr")
 MASKED_SCORE = -1e30
 FLOOR = -1e29
 MESH = pl.DeviceIdType.MESH
@@ -372,13 +381,12 @@
     a_s, a_r, xq_s, xq_r, o_s, o_r, l_s, l_r,
     b_s, b_r, bl_s, bl_r, g_s, g_r, d_s, d_r,
 ):
-    nth, tt, hl, ns, Lb, hd, G = dims
+    parts, hl, ns, Lb, hd, G = dims
     n_tp, n_seq = lax.axis_size("tp"), lax.axis_size("seq")
     me_t, me_s = lax.axis_index("tp"), lax.axis_index("seq")
     per_tp = out_ref.shape[0]
-    nc = per_tp * nth
-    T = nth * tt
-    rows = G * tt
+    nc = len(parts)
+    T = out_ref.shape[1]
     columns = w_ref.shape[1]
     half = me_t // 2
     partner = me_t + 1 - 2 * (me_t % 2)
@@ -390,9 +398,6 @@
     scale = math.log2(math.e) / math.sqrt(hd)
     bf, f32 = jnp.bfloat16, jnp.float32
 
-    def part(c):
-        return c // nth, c % nth
-
     def to(axis, target, src, dst, send, recv):
         return pltpu.make_async_remote_copy(
             src_ref=src, dst_ref=dst, send_sem=send, recv_sem=recv,
@@ -411,17 +416,17 @@
     via_a = [block_to(c, 3, far_inner, partner) for c in range(nc)]
     via_b = [block_to(c, 4, far_outer, partner) for c in range(nc)]
     column = lambda k: lax.rem(me_s + k, n_seq)
-    xsends = ring(lambda c, k: to("seq", column(k), xs.at[c, k], xr.at[c, k], xq_s.at[c, k], xq_r.at[c, k]))
-    osends = ring(lambda c, k: to("seq", column(k), osend.at[c, k], orecv[c].at[k], o_s.at[c, k], o_r.at[c, k]))
-    lsends = ring(lambda c, k: to("seq", column(k), lsend.at[c, k], lrecv[c].at[k], l_s.at[c, k], l_r.at[c, k]))
-    gsends = ring(lambda c, k: to("seq", column(k), xg.at[c, 0], xg.at[c, k], g_s.at[c, k], g_r.at[c, k]))
+    xsends = ring(lambda c, k: to("seq", column(k), xs[c].at[k], xr[c].at[k], xq_s.at[c, k], xq_r.at[c, k]))
+    osends = ring(lambda c, k: to("seq", column(k), osend[c].at[k], orecv[c].at[k], o_s.at[c, k], o_r.at[c, k]))
+    lsends = ring(lambda c, k: to("seq", column(k), lsend[c].at[k], lrecv[c].at[k], l_s.at[c, k], l_r.at[c, k]))
+    gsends = ring(lambda c, k: to("seq", column(k), xg[c].at[0], xg[c].at[k], g_s.at[c, k], g_r.at[c, k]))
 
     def swap(c, send, mid, out, s, r):
         return dict(
-            pair=to("tp", partner, send.at[c, 0], out.at[c, 0], s.at[c, 0], r.at[c, 0]),
-            lift=[to("tp", partner, send.at[c, i], mid.at[c, i - 1], s.at[c, i], r.at[c, i]) for i in (1, 2)],
+            pair=to("tp", partner, send[c].at[0], out[c].at[0], s.at[c, 0], r.at[c, 0]),
+            lift=[to("tp", partner, send[c].at[i], mid[c].at[i - 1], s.at[c, i], r.at[c, i]) for i in (1, 2)],
             cross=[
-                to("tp", target, send.at[c, i], out.at[c, 1], s.at[c, 2 + i], r.at[c, 3])
+                to("tp", target, send[c].at[i], out[c].at[1], s.at[c, 2 + i], r.at[c, 3])
                 for i, target in ((1, far_inner), (2, far_outer))
             ],
         )
@@ -430,11 +435,11 @@
     dz = [(swap(c, ds, dm, dr, d_s, d_r),) for c in range(nc)]
 
     def own_blocks(c):
-        x, th = part(c)
+        x, t0, tt = parts[c]
         for j in range(hl):
             for g in range(G):
                 yield pltpu.make_async_copy(
-                    q_hbm.at[me_s * per_tp + x, pl.ds(th * tt, tt), pl.ds((j * G + g) * hd, hd)],
+                    q_hbm.at[me_s * per_tp + x, pl.ds(t0, tt), pl.ds((j * G + g) * hd, hd)],
                     az[c].at[me_t, j, g],
                     q_sem.at[c],
                 )
@@ -472,16 +477,17 @@
             target = xr if k == 0 else xs
             for j in range(ns):
                 head = hos[column(k) * ns + j]
-                target[c, k, j] = az[c][head // hl, head % hl]
+                target[c][k, j] = az[c][head // hl, head % hl]
             if k:
                 xsends[c][k - 1].start()
 
     def attend_pair(c, k, slot):
-        x, th = part(c)
+        x, t0, tt = parts[c]
+        rows = G * tt
         seq = column(k) * per_tp + x
-        queries = xr[c, (n_seq - k) % n_seq, slot].reshape(rows, hd)
+        queries = xr[c][(n_seq - k) % n_seq, slot].reshape(rows, hd)
         visible_end = lens[seq] - me_t * Lb
-        limits = visible_end - T + th * tt + lax.broadcasted_iota(jnp.int32, (1, rows), 1) % tt
+        limits = visible_end - T + t0 + lax.broadcasted_iota(jnp.int32, (1, rows), 1) % tt
         top = jnp.full((1, rows), FLOOR, f32)
         for i in range(Lb // block):
             s = lax.dot_general(
@@ -492,12 +498,12 @@
             )
             pos = i * block + lax.broadcasted_iota(jnp.int32, (block, 1), 0)
             s = jnp.where(pos <= limits, s * scale, MASKED_SCORE)
-            scores[i * block : (i + 1) * block, :] = s
+            scores[i * block : (i + 1) * block, :rows] = s
             top = jnp.maximum(top, jnp.max(s, axis=0, keepdims=True))
         total = jnp.zeros((1, rows), f32)
         out = jnp.zeros((hd, rows), f32)
         for i in range(Lb // block):
-            w = jnp.exp2(scores[i * block : (i + 1) * block, :] - top)
+            w = jnp.exp2(scores[i * block : (i + 1) * block, :rows] - top)
             total = total + jnp.sum(w, axis=0, keepdims=True)
             out = out + lax.dot_general(
                 kv_ref[slot, seq, i * block : (i + 1) * block, hd:],
@@ -506,19 +512,18 @@
                 preferred_element_type=f32,
             )
         total = jnp.maximum(total, 1e-30)
-        o_to = orecv[c].at[0] if k == 0 else osend.at[c, k]
-        l_to = lrecv[c].at[0] if k == 0 else lsend.at[c, k]
+        o_to = orecv[c].at[0] if k == 0 else osend[c].at[k]
+        l_to = lrecv[c].at[0] if k == 0 else lsend[c].at[k]
         o_to[slot] = (out / total).astype(bf)
         l_to[slot] = top + jnp.log2(total)
 
-    def attend(c):
-        for copy in xsends[c]:
-            copy.wait_recv()
-        for k in list(range(1, n_seq)) + [0]:
-            lax.fori_loop(0, ns, lambda slot, _: (attend_pair(c, k, slot), 0)[1], 0)
-            if k:
-                osends[c][k - 1].start()
-                lsends[c][k - 1].start()
+    def attend(c, k):
+        if k:
+            xsends[c][n_seq - k - 1].wait_recv()
+        lax.fori_loop(0, ns, lambda slot, _: (attend_pair(c, k, slot), 0)[1], 0)
+        if k:
+            osends[c][k - 1].start()
+            lsends[c][k - 1].start()
 
     def picked(c, plane, j):
         head = plane * hl + j
@@ -541,8 +546,8 @@
     def put(c, i, plane):
         for j in range(hl):
             o, l = picked(c, plane, j)
-            bs[c, i, j] = o
-            bls[c, i, j] = l
+            bs[c][i, j] = o
+            bls[c][i, j] = l
 
     def part_send(c):
         for copy in osends[c] + lsends[c]:
@@ -566,41 +571,43 @@
                 for z in bz[c]:
                     z["lift"][i - 1].wait_recv()
                 for j in range(hl):
-                    o, l = merged([picked(c, plane, j), (bm[c, i - 1, j], blm[c, i - 1, j])])
-                    bs[c, i, j] = o.astype(bf)
-                    bls[c, i, j] = l
+                    o, l = merged([picked(c, plane, j), (bm[c][i - 1, j], blm[c][i - 1, j])])
+                    bs[c][i, j] = o.astype(bf)
+                    bls[c][i, j] = l
                 for z in bz[c]:
                     z["cross"][i - 1].start()
 
     def part_end(c):
+        tt = parts[c][2]
         for z in bz[c]:
             z["pair"].wait_recv()
             z["cross"][0].wait_recv()
         for j in range(hl):
-            o, _ = merged([picked(c, me_t, j)] + [(br[c, i, j], blr[c, i, j]) for i in range(2)])
+            o, _ = merged([picked(c, me_t, j)] + [(br[c][i, j], blr[c][i, j]) for i in range(2)])
             turned = o.T.astype(bf)
             for g in range(G):
                 at = (j * G + g) * hd
-                xg[c, 0, :, at : at + hd] = turned[g * tt : (g + 1) * tt]
+                xg[c][0, :, at : at + hd] = turned[g * tt : (g + 1) * tt]
         for copy in gsends[c]:
             copy.start()
 
     tile = math.gcd(columns, 512)
 
     def project(c):
+        tt = parts[c][2]
         for copy in gsends[c]:
             copy.wait_recv()
         planes = [me_t, partner, far_inner, far_outer]
         lhs = jnp.concatenate(
-            [xg[c, lax.rem(me_s + n_seq - p, n_seq)] for p in planes], axis=0
+            [xg[c][lax.rem(me_s + n_seq - p, n_seq)] for p in planes], axis=0
         )
 
         def column_tile(i, _):
             at = pl.ds(pl.multiple_of(i * tile, tile), tile)
             product = jnp.dot(lhs, w_ref[:, at], preferred_element_type=f32)
-            own[c, :, at] = product[:tt]
+            own[c][:, at] = product[:tt]
             for i in range(3):
-                ds[c, i, :, at] = product[(i + 1) * tt : (i + 2) * tt].astype(bf)
+                ds[c][i, :, at] = product[(i + 1) * tt : (i + 2) * tt].astype(bf)
             return 0
 
         lax.fori_loop(0, columns // tile, column_tile, 0)
@@ -619,16 +626,16 @@
         def _():
             for i in (2, 1):
                 z["lift"][i - 1].wait_recv()
-                ds[c, i] = (ds[c, i].astype(f32) + dm[c, i - 1].astype(f32)).astype(bf)
+                ds[c][i] = (ds[c][i].astype(f32) + dm[c][i - 1].astype(f32)).astype(bf)
                 z["cross"][i - 1].start()
 
     def sum_end(c):
-        x, th = part(c)
+        x, t0, tt = parts[c]
         z = dz[c][0]
         z["pair"].wait_recv()
         z["cross"][0].wait_recv()
-        total = own[c] + dr[c, 0].astype(f32) + dr[c, 1].astype(f32)
-        out_ref[x, th * tt : (th + 1) * tt] = total.astype(bf)
+        total = own[c][...] + dr[c][0].astype(f32) + dr[c][1].astype(f32)
+        out_ref[x, t0 : t0 + tt] = total.astype(bf)
 
     step = math.gcd(Lb, 128)
     turns = Lb // step
@@ -659,11 +666,16 @@
     greet(("tp", "seq"))
 
     run = dict(
-        q=ask_own, ra=relay_a, rb=relay_b, sp=spread, at=attend, bs=part_send, bj=part_join,
-        be=part_end, pr=project, dj=sum_join, de=sum_end, kv=split, w=lambda _: load.wait(),
+        q=ask_own, ra=relay_a, rb=relay_b, sp=spread, bs=part_send, bj=part_join, be=part_end,
+        pr=project, dj=sum_join, de=sum_end, kv=split,
+        a0=lambda c: attend(c, 0), a1=lambda c: attend(c, 1),
+        a2=lambda c: attend(c, 2), a3=lambda c: attend(c, 3),
     )
-    for name, c in order_of(nc, n_b):
-        run[name](c)
+    for entry in ORDER:
+        name, c = entry.rsplit(".", 1)
+        if entry == FIRST_PROJECT:
+            load.wait()
+        run[name](int(c))
 
     for c in range(nc):
         own_p[c].wait_send()
@@ -687,22 +699,7 @@
                     copy.wait_send()
 
 
-def order_of(nc, n_b):
-    steps = ["ra", "rb", "sp", "at", "bs", "bj", "be", "pr", "dj", "de"]
-    after = dict(zip(steps, AFTER))
-    plan = []
-    for c in range(nc):
-        for place, name in enumerate(steps):
-            plan.append((c * PERIOD + after[name], place, name, c))
-        if c:
-            plan.append(((c - 1) * PERIOD + after["ra"] + 0.1, 0, "q", c))
-    for i in range(n_b):
-        plan.append((SPLIT_AT[i * len(SPLIT_AT) // n_b], 0, "kv", i))
-    plan.append((after["pr"] - 0.01, 0, "w", 0))
-    return [("q", 0)] + [(name, c) for _, _, name, c in sorted(plan, key=lambda e: (e[0], -e[1]))]
-
-
-def line_call(query, cache, head_of_slot, lengths, out_weight, nth):
+def line_call(query, cache, head_of_slot, lengths, out_weight, cuts):
     n_seq, n_tp = lax.axis_size("seq"), lax.axis_size("tp")
     G = HQ // KVH
     B, T, _ = query.shape
@@ -710,9 +707,14 @@
     hd = hd2 // 2
     hl = KVH // n_tp
     per_tp = B // n_tp
-    tt = T // nth
-    nc = per_tp * nth
-    rows = G * tt
+    parts = []
+    for x in range(per_tp):
+        t0 = 0
+        for tt in cuts[x % len(cuts)]:
+            parts.append((x, t0, tt))
+            t0 += tt
+    sizes = [tt for _, _, tt in parts]
+    nc = len(parts)
     columns = out_weight.shape[1]
     bf, f32 = jnp.bfloat16, jnp.float32
     dma = pltpu.SemaphoreType.DMA
@@ -720,7 +722,7 @@
     anywhere = pl.BlockSpec(memory_space=pl.ANY)
     smem = pl.BlockSpec(memory_space=pltpu.SMEM)
     return pl.pallas_call(
-        functools.partial(line_kernel, (nth, tt, hl, ns, Lb, hd, G)),
+        functools.partial(line_kernel, (tuple(parts), hl, ns, Lb, hd, G)),
         out_shape=jax.ShapeDtypeStruct((per_tp, T, columns), bf),
         in_specs=[smem, smem, anywhere, anywhere, anywhere],
         out_specs=pl.BlockSpec(memory_space=pltpu.VMEM),
@@ -728,20 +730,22 @@
             v(cache.shape, bf),
             v((ns, B, Lb, 2 * hd), bf),
             v(out_weight.shape, bf),
-            [v((n_tp, hl, G, tt, hd), bf)] * nc,
-            v((nc, n_seq, ns, G, tt, hd), bf),
-            v((nc, n_seq, ns, G, tt, hd), bf),
-            v((nc, n_seq, ns, hd, rows), bf),
-            [v((n_seq, ns, hd, rows), bf)] * nc,
-            v((nc, n_seq, ns, 1, rows), f32),
-            [v((n_seq, ns, 1, rows), f32)] * nc,
-            v((Lb, rows), f32),
-            v((nc, 3, hl, hd, rows), bf), v((nc, 3, hl, 1, rows), f32),
-            v((nc, 2, hl, hd, rows), bf), v((nc, 2, hl, 1, rows), f32),
-            v((nc, 2, hl, hd, rows), bf), v((nc, 2, hl, 1, rows), f32),
-            v((nc, n_seq, tt, hl * G * hd), bf),
-            v((nc, tt, columns), f32),
-            v((nc, 3, tt, columns), bf), v((nc, 2, tt, columns), bf), v((nc, 2, tt, columns), bf),
+            [v((n_tp, hl, G, tt, hd), bf) for tt in sizes],
+            [v((n_seq, ns, G, tt, hd), bf) for tt in sizes],
+            [v((n_seq, ns, G, tt, hd), bf) for tt in sizes],
+            [v((n_seq, ns, hd, G * tt), bf) for tt in sizes],
+            [v((n_seq, ns, hd, G * tt), bf) for tt in sizes],
+            [v((n_seq, ns, 1, G * tt), f32) for tt in sizes],
+            [v((n_seq, ns, 1, G * tt), f32) for tt in sizes],
+            v((Lb, G * max(sizes)), f32),
+            [v((3, hl, hd, G * tt), bf) for tt in sizes], [v((3, hl, 1, G * tt), f32) for tt in sizes],
+            [v((2, hl, hd, G * tt), bf) for tt in sizes], [v((2, hl, 1, G * tt), f32) for tt in sizes],
+            [v((2, hl, hd, G * tt), bf) for tt in sizes], [v((2, hl, 1, G * tt), f32) for tt in sizes],
+            [v((n_seq, tt, hl * G * hd), bf) for tt in sizes],
+            [v((tt, columns), f32) for tt in sizes],
+            [v((3, tt, columns), bf) for tt in sizes],
+            [v((2, tt, columns), bf) for tt in sizes],
+            [v((2, tt, columns), bf) for tt in sizes],
             dma((B,)), dma(()), dma((nc,)),
             dma((nc, 5)), dma((nc, 5)),
             dma((nc, n_seq)), dma((nc, n_seq)),
@@ -766,9 +770,9 @@
     hd = hd2 // 2
     hl = KVH // n_tp
     per_tp = B // n_tp
-    nth = math.gcd(TOKEN_CUTS, T)
-    if n_tp == n_seq == 4 and HQ * hd == n_tp * width and T // nth % 16 == 0:
-        return line_call(query, cache, head_of_slot, lengths, out_weight, nth)
+    fits = all(sum(cut) == T for cut in CUTS) and len(CUTS) == per_tp
+    if n_tp == n_seq == 4 and HQ * hd == n_tp * width and fits:
+        return line_call(query, cache, head_of_slot, lengths, out_weight, CUTS)
     nc = math.gcd(CHUNKS, per_tp)
     bq = per_tp // nc
     nsq = n_tp * bq // n_seq

time: 130 us -> 117 us (0.900)
  Pallas kernels: 128 us -> 115 us
    pallas_call x1, Pallas kernels: 128 us -> 115 us  [line_call(): pl.pallas_call(functools.partial(line_kernel, (tuple(parts), hl, ns, Lb,...]
where the time goes in v2:
time: 117 us
  Pallas kernels  115 us (98%)
  local copies, waits for them, and re-layouts  1.88 us (2%)
    pallas_call x1, Pallas kernels, line_call(): pl.pallas_call(functools.partial(line_kernel, (tuple(parts), hl, ns, Lb,...  115 us

profile of v2, /device:TPU:0, one launch (start us, length us, event | category | flops | bytes accessed | tf_op | source)
XLA Modules:
  0.0 116.9 jit_solution(1884729266888407375)
XLA Ops:
  0.0 115.0 %shard_map.55 = bf16[2,64,2048]{2,1,0:T(8,128)(2,1)} custom-call(s32[8]{0:T(128)} %hos.1, s32[8]{0:T(128)} %lens.1, bf16[8,64,2048]{2,1,0:T(8,128)(2,1)} %q_hbm.1, bf16[8,1024,2,256]{3,2,1,0:T(2,128)(2,1)} %kv_hbm.1, bf16[2048,2048]{1,0:T(8,128)(2,1)} %w_hbm.1), custom_call_target="tpu_custom_call" | custom-call | tf_op jit(solution)/shard_map/pallas_call | solution.py:724
  115.0 1.9 %copy.7 = bf16[2,64,2048]{2,1,0:T(8,128)(2,1)} copy(bf16[2,64,2048]{2,1,0:T(8,128)(2,1)} %shard_map.55) | data formatting | bytes 1048576

commit v3 on v2

--- a/solution.py
+++ b/solution.py
@@ -11,17 +11,20 @@
 HQ = 64
 KVH = 8
 CHUNKS = 2
-CUTS = ((16, 32, 16), (16, 32, 16))
+SLOTS = 3
+CUTS = ((16, 16, 16, 16), (16, 32, 16))
 ORDER = (
-    "q.0", "q.1", "kv.0", "ra.0", "kv.1", "ra.1", "kv.2", "rb.0", "kv.3", "rb.1", "q.5", "q.2",
-    "kv.4", "sp.0", "q.4", "a0.0", "sp.1", "a0.1", "ra.2", "a1.0", "a2.0", "ra.4", "kv.5", "a1.1",
-    "rb.2", "a3.0", "a2.1", "q.3", "rb.4", "ra.5", "sp.2", "a3.1", "bs.0", "kv.6", "sp.4", "bj.0",
-    "a0.2", "ra.3", "kv.7", "rb.5", "bs.1", "a0.4", "a1.2", "a2.2", "a3.2", "be.0", "bj.1",
-    "a1.4", "rb.3", "a2.4", "bs.2", "a3.4", "pr.0", "be.1", "sp.5", "bj.2", "sp.3", "a0.3",
-    "bs.4", "dj.0", "pr.1", "a0.5", "a1.5", "a2.5", "bj.4", "a1.3", "a2.3", "a3.5", "a3.3",
-    "dj.1", "bs.5", "be.2", "bs.3", "be.4", "pr.2", "bj.3", "bj.5", "pr.4", "dj.2", "be.3",
-    "be.5", "dj.4", "de.1", "pr.3", "de.0", "pr.5", "dj.3", "de.4", "de.2", "dj.5", "de.3",
-    "de.5",
+    "kv.0", "hello.0", "q.0", "q.1", "kv.1", "kv.2", "ra.0", "ra.1", "kv.3", "rb.0", "kv.4",
+    "rb.1", "q.2", "kv.5", "q.3", "kv.6", "sp.0", "kv.7", "ra.2", "ra.3", "sp.1", "a0.0", "a1.0",
+    "rb.2", "q.4", "a2.0", "a0.1", "rb.3", "ra.4", "a3.0", "a1.1", "q.5", "sp.2", "a0.2", "a2.1",
+    "a3.1", "bs.0", "rb.4", "sp.3", "kv.8", "kv.9", "a1.2", "ra.5", "a2.2", "bj.0", "a3.2",
+    "bs.1", "q.6", "a0.3", "a1.3", "a2.3", "bj.1", "a3.3", "kv.10", "rb.5", "sp.4", "kv.11",
+    "kv.12", "be.0", "bs.2", "bs.3", "kv.13", "kv.14", "be.1", "kv.15", "a0.4", "bj.2", "sp.5",
+    "ra.6", "a1.4", "pr.0", "bj.3", "pr.1", "a2.4", "a3.4", "a0.5", "be.2", "a1.5", "dj.0",
+    "a2.5", "rb.6", "dj.1", "bs.4", "a3.5", "pr.2", "sp.6", "be.3", "bj.4", "bs.5", "a0.6",
+    "a1.6", "a2.6", "a3.6", "bj.5", "dj.2", "pr.3", "be.4", "dj.3", "be.5", "bs.6", "bj.6",
+    "pr.4", "dj.4", "de.3", "pr.5", "be.6", "de.2", "dj.5", "de.0", "pr.6", "de.4", "de.1",
+    "dj.6", "de.5", "de.6",
 )
 FIRST_PROJECT = next(e for e in ORDER if e[:2] == "pr")
 MASKED_SCORE = -1e30
@@ -373,20 +376,34 @@
     )(slot_of_head, att, weight)
 
 
+def greet_start(axes):
+    barrier = pltpu.get_barrier_semaphore()
+    total = 0
+    for axis in axes:
+        n = lax.axis_size(axis)
+        me = lax.axis_index(axis)
+        for k in range(1, n):
+            pl.semaphore_signal(
+                barrier, inc=1, device_id={axis: lax.rem(me + k, n)}, device_id_type=MESH
+            )
+            total += 1
+    return total
+
+
 def line_kernel(
-    dims, hos, lens, q_hbm, kv_hbm, w_hbm, out_ref,
+    dims, hos, lens, q_hbm, kv_hbm, w_hbm, out_hbm,
     raw, kv_ref, w_ref, az, xs, xr, osend, orecv, lsend, lrecv, scores,
     bs, bls, bm, blm, br, blr, xg, own, ds, dm, dr,
     kv_sem, w_sem, q_sem,
     a_s, a_r, xq_s, xq_r, o_s, o_r, l_s, l_r,
-    b_s, b_r, bl_s, bl_r, g_s, g_r, d_s, d_r,
+    b_s, b_r, bl_s, bl_r, g_s, g_r, d_s, d_r, out_ref, out_sem,
 ):
     parts, hl, ns, Lb, hd, G = dims
     n_tp, n_seq = lax.axis_size("tp"), lax.axis_size("seq")
     me_t, me_s = lax.axis_index("tp"), lax.axis_index("seq")
-    per_tp = out_ref.shape[0]
+    per_tp = out_hbm.shape[0]
     nc = len(parts)
-    T = out_ref.shape[1]
+    T = out_hbm.shape[1]
     columns = w_ref.shape[1]
     half = me_t // 2
     partner = me_t + 1 - 2 * (me_t % 2)
@@ -405,34 +422,60 @@
         )
 
     def ring(target_of):
-        return [[target_of(c, k) for k in range(1, n_seq)] for c in range(nc)]
-
-    def block_to(c, i, plane, target):
-        return to("tp", target, az[c].at[plane], az[c].at[plane], a_s.at[c, i], a_r.at[c, i])
-
-    own_p = [block_to(c, 0, me_t, partner) for c in range(nc)]
-    own_f = [block_to(c, 1, me_t, far_inner) for c in range(nc)]
-    via_f = [block_to(c, 2, partner, far_inner) for c in range(nc)]
-    via_a = [block_to(c, 3, far_inner, partner) for c in range(nc)]
-    via_b = [block_to(c, 4, far_outer, partner) for c in range(nc)]
+        return {k: [target_of(c, k) for c in range(nc)] for k in range(1, n_seq)}
+
+    turn_of = {}
+    for entry in ORDER:
+        name, c = entry.rsplit(".", 1)
+        turn_of.setdefault(name, []).append(int(c))
+
+    def slot(name, c):
+        return turn_of[name].index(c) % SLOTS
+
+    def begin(name, c, copies):
+        turn = turn_of[name].index(c)
+        if turn >= SLOTS:
+            copies[turn_of[name][turn - SLOTS]].wait_send()
+        copies[c].start()
+
+    def finish(name, copies):
+        for c in turn_of[name][-SLOTS:]:
+            copies[c].wait_send()
+
+    def block_to(c, name, i, r, plane, target):
+        return to(
+            "tp", target, az[c].at[plane], az[c].at[plane], a_s.at[slot(name, c), i], a_r.at[c, r]
+        )
+
+    own_p = [block_to(c, "q", 0, 0, me_t, partner) for c in range(nc)]
+    own_f = [block_to(c, "q", 1, 1, me_t, far_inner) for c in range(nc)]
+    via_f = [block_to(c, "ra", 2, 2, partner, far_inner) for c in range(nc)]
+    via_a = [block_to(c, "ra", 3, 1, far_inner, partner) for c in range(nc)]
+    via_b = [block_to(c, "rb", 4, 2, far_outer, partner) for c in range(nc)]
     column = lambda k: lax.rem(me_s + k, n_seq)
-    xsends = ring(lambda c, k: to("seq", column(k), xs[c].at[k], xr[c].at[k], xq_s.at[c, k], xq_r.at[c, k]))
-    osends = ring(lambda c, k: to("seq", column(k), osend[c].at[k], orecv[c].at[k], o_s.at[c, k], o_r.at[c, k]))
-    lsends = ring(lambda c, k: to("seq", column(k), lsend[c].at[k], lrecv[c].at[k], l_s.at[c, k], l_r.at[c, k]))
-    gsends = ring(lambda c, k: to("seq", column(k), xg[c].at[0], xg[c].at[k], g_s.at[c, k], g_r.at[c, k]))
-
-    def swap(c, send, mid, out, s, r):
+    xsends = ring(lambda c, k: to("seq", column(k), xs[c].at[k], xr[c].at[k], xq_s.at[slot("sp", c), k - 1], xq_r.at[c, k - 1]))
+    osends = ring(lambda c, k: to("seq", column(k), osend[c].at[k], orecv[c].at[k], o_s.at[slot(f"a{k}", c), k - 1], o_r.at[c, k - 1]))
+    lsends = ring(lambda c, k: to("seq", column(k), lsend[c].at[k], lrecv[c].at[k], l_s.at[slot(f"a{k}", c), k - 1], l_r.at[c, k - 1]))
+    gsends = ring(lambda c, k: to("seq", column(k), xg[c].at[0], xg[c].at[k], g_s.at[slot("be", c), k - 1], g_r.at[c, k - 1]))
+
+    def swap(first, second, send, mid, out, s, r):
+        def one(c, name, i, r_i, target, dst):
+            return to("tp", target, send[c].at[i], dst, s.at[slot(name, c), i], r.at[c, r_i])
+
         return dict(
-            pair=to("tp", partner, send[c].at[0], out[c].at[0], s.at[c, 0], r.at[c, 0]),
-            lift=[to("tp", partner, send[c].at[i], mid[c].at[i - 1], s.at[c, i], r.at[c, i]) for i in (1, 2)],
-            cross=[
-                to("tp", target, send[c].at[i], out[c].at[1], s.at[c, 2 + i], r.at[c, 3])
+            pair=[one(c, first, 0, 0, partner, out[c].at[0]) for c in range(nc)],
+            lift={i: [one(c, first, i, i, partner, mid[c].at[i - 1]) for c in range(nc)] for i in (1, 2)},
+            cross={
+                i: [
+                    to("tp", target, send[c].at[i], out[c].at[1], s.at[slot(second, c), 2 + i], r.at[c, 3])
+                    for c in range(nc)
+                ]
                 for i, target in ((1, far_inner), (2, far_outer))
-            ],
+            },
         )
 
-    bz = [(swap(c, bs, bm, br, b_s, b_r), swap(c, bls, blm, blr, bl_s, bl_r)) for c in range(nc)]
-    dz = [(swap(c, ds, dm, dr, d_s, d_r),) for c in range(nc)]
+    bz = (swap("bs", "bj", bs, bm, br, b_s, b_r), swap("bs", "bj", bls, blm, blr, bl_s, bl_r))
+    dz = (swap("pr", "dj", ds, dm, dr, d_s, d_r),)
 
     def own_blocks(c):
         x, t0, tt = parts[c]
@@ -446,25 +489,25 @@
 
     def ask_own(c):
         pltpu.make_async_copy(az[c].at[me_t], az[c].at[me_t], q_sem.at[c]).wait()
-        own_p[c].start()
+        begin("q", c, own_p)
 
         @pl.when(inner)
         def _():
-            own_f[c].start()
+            begin("q", c, own_f)
 
     def relay_a(c):
         @pl.when(inner)
         def _():
             own_p[c].wait_recv()
-            via_f[c].start()
+            begin("ra", c, via_f)
             own_f[c].wait_recv()
-            via_a[c].start()
+            begin("ra", c, via_a)
 
     def relay_b(c):
         @pl.when(inner)
         def _():
             via_f[c].wait_recv()
-            via_b[c].start()
+            begin("rb", c, via_b)
 
     def spread(c):
         @pl.when(outer)
@@ -479,7 +522,7 @@
                 head = hos[column(k) * ns + j]
                 target[c][k, j] = az[c][head // hl, head % hl]
             if k:
-                xsends[c][k - 1].start()
+                begin("sp", c, xsends[k])
 
     def attend_pair(c, k, slot):
         x, t0, tt = parts[c]
@@ -519,11 +562,11 @@
 
     def attend(c, k):
         if k:
-            xsends[c][n_seq - k - 1].wait_recv()
+            xsends[n_seq - k][c].wait_recv()
         lax.fori_loop(0, ns, lambda slot, _: (attend_pair(c, k, slot), 0)[1], 0)
         if k:
-            osends[c][k - 1].start()
-            lsends[c][k - 1].start()
+            begin(f"a{k}", c, osends[k])
+            begin(f"a{k}", c, lsends[k])
 
     def picked(c, plane, j):
         head = plane * hl + j
@@ -550,53 +593,54 @@
             bls[c][i, j] = l
 
     def part_send(c):
-        for copy in osends[c] + lsends[c]:
-            copy.wait_recv()
+        for k in range(1, n_seq):
+            osends[k][c].wait_recv()
+            lsends[k][c].wait_recv()
 
         @pl.when(outer)
         def _():
-            for i, plane in ((1, far_inner), (2, far_outer)):
+            for i, plane in ((2, far_outer), (1, far_inner)):
                 put(c, i, plane)
-                for z in bz[c]:
-                    z["lift"][i - 1].start()
+                for z in bz:
+                    begin("bs", c, z["lift"][i])
 
         put(c, 0, partner)
-        for z in bz[c]:
-            z["pair"].start()
+        for z in bz:
+            begin("bs", c, z["pair"])
 
     def part_join(c):
         @pl.when(inner)
         def _():
             for i, plane in ((2, far_outer), (1, far_inner)):
-                for z in bz[c]:
-                    z["lift"][i - 1].wait_recv()
+                for z in bz:
+                    z["lift"][i][c].wait_recv()
                 for j in range(hl):
                     o, l = merged([picked(c, plane, j), (bm[c][i - 1, j], blm[c][i - 1, j])])
                     bs[c][i, j] = o.astype(bf)
                     bls[c][i, j] = l
-                for z in bz[c]:
-                    z["cross"][i - 1].start()
+                for z in bz:
+                    begin("bj", c, z["cross"][i])
 
     def part_end(c):
         tt = parts[c][2]
-        for z in bz[c]:
-            z["pair"].wait_recv()
-            z["cross"][0].wait_recv()
+        for z in bz:
+            z["pair"][c].wait_recv()
+            z["cross"][1][c].wait_recv()
         for j in range(hl):
             o, _ = merged([picked(c, me_t, j)] + [(br[c][i, j], blr[c][i, j]) for i in range(2)])
             turned = o.T.astype(bf)
             for g in range(G):
                 at = (j * G + g) * hd
                 xg[c][0, :, at : at + hd] = turned[g * tt : (g + 1) * tt]
-        for copy in gsends[c]:
-            copy.start()
+        for k in range(1, n_seq):
+            begin("be", c, gsends[k])
 
     tile = math.gcd(columns, 512)
 
     def project(c):
         tt = parts[c][2]
-        for copy in gsends[c]:
-            copy.wait_recv()
+        for k in range(1, n_seq):
+            gsends[k][c].wait_recv()
         planes = [me_t, partner, far_inner, far_outer]
         lhs = jnp.concatenate(
             [xg[c][lax.rem(me_s + n_seq - p, n_seq)] for p in planes], axis=0
@@ -614,28 +658,29 @@
 
         @pl.when(outer)
         def _():
-            for copy in dz[c][0]["lift"]:
-                copy.start()
-
-        dz[c][0]["pair"].start()
+            for i in (2, 1):
+                begin("pr", c, dz[0]["lift"][i])
+
+        begin("pr", c, dz[0]["pair"])
 
     def sum_join(c):
-        z = dz[c][0]
+        z = dz[0]
 
         @pl.when(inner)
         def _():
             for i in (2, 1):
-                z["lift"][i - 1].wait_recv()
+                z["lift"][i][c].wait_recv()
                 ds[c][i] = (ds[c][i].astype(f32) + dm[c][i - 1].astype(f32)).astype(bf)
-                z["cross"][i - 1].start()
+                begin("dj", c, z["cross"][i])
 
     def sum_end(c):
         x, t0, tt = parts[c]
-        z = dz[c][0]
-        z["pair"].wait_recv()
-        z["cross"][0].wait_recv()
+        z = dz[0]
+        z["pair"][c].wait_recv()
+        z["cross"][1][c].wait_recv()
         total = own[c][...] + dr[c][0].astype(f32) + dr[c][1].astype(f32)
         out_ref[x, t0 : t0 + tt] = total.astype(bf)
+        gives[c].start()
 
     step = math.gcd(Lb, 128)
     turns = Lb // step
@@ -644,8 +689,11 @@
     fetches = [pltpu.make_async_copy(kv_hbm.at[b], raw.at[b], kv_sem.at[b]) for b in range(n_b)]
 
     def split(index):
-        b = seq_order[index]
-        fetches[b].wait()
+        b = seq_order[index // 2]
+        if index % 2 == 0:
+            fetches[b].wait()
+        first = index % 2 * (turns // 2)
+        last = turns if index % 2 else turns // 2
 
         def turn(i, _):
             at = pl.ds(pl.multiple_of(i * step, step), step)
@@ -653,9 +701,15 @@
                 kv_ref[slot, b, at, :] = raw[b, at, slot, :]
             return 0
 
-        lax.fori_loop(0, turns, turn, 0)
+        lax.fori_loop(first, last, turn, 0)
 
     load = pltpu.make_async_copy(w_hbm, w_ref, w_sem)
+    gives = [
+        pltpu.make_async_copy(
+            out_ref.at[x, pl.ds(t0, tt)], out_hbm.at[x, pl.ds(t0, tt)], out_sem.at[c]
+        )
+        for c, (x, t0, tt) in enumerate(parts)
+    ]
 
     for c in range(nc):
         for copy in own_blocks(c):
@@ -663,9 +717,10 @@
     for b in seq_order:
         fetches[b].start()
     load.start()
-    greet(("tp", "seq"))
+    signalled = greet_start(("tp", "seq"))
 
     run = dict(
+        hello=lambda _: pl.semaphore_wait(pltpu.get_barrier_semaphore(), signalled),
         q=ask_own, ra=relay_a, rb=relay_b, sp=spread, bs=part_send, bj=part_join, be=part_end,
         pr=project, dj=sum_join, de=sum_end, kv=split,
         a0=lambda c: attend(c, 0), a1=lambda c: attend(c, 1),
@@ -677,26 +732,34 @@
             load.wait()
         run[name](int(c))
 
-    for c in range(nc):
-        own_p[c].wait_send()
-        for copy in xsends[c] + osends[c] + lsends[c] + gsends[c]:
-            copy.wait_send()
-        for z in bz[c] + dz[c]:
-            z["pair"].wait_send()
-
-        @pl.when(outer)
-        def _():
-            for z in bz[c] + dz[c]:
-                for copy in z["lift"]:
-                    copy.wait_send()
-
-        @pl.when(inner)
-        def _():
-            for copy in (own_f[c], via_f[c], via_a[c], via_b[c]):
-                copy.wait_send()
-            for z in bz[c] + dz[c]:
-                for copy in z["cross"]:
-                    copy.wait_send()
+    finish("q", own_p)
+    for k in range(1, n_seq):
+        finish("sp", xsends[k])
+        finish(f"a{k}", osends[k])
+        finish(f"a{k}", lsends[k])
+        finish("be", gsends[k])
+    for name, zs in (("bs", bz), ("pr", dz)):
+        for z in zs:
+            finish(name, z["pair"])
+
+    @pl.when(outer)
+    def _():
+        for name, zs in (("bs", bz), ("pr", dz)):
+            for z in zs:
+                finish(name, z["lift"][1])
+                finish(name, z["lift"][2])
+
+    @pl.when(inner)
+    def _():
+        for name, copies in (("q", own_f), ("ra", via_f), ("ra", via_a), ("rb", via_b)):
+            finish(name, copies)
+        for name, zs in (("bj", bz), ("dj", dz)):
+            for z in zs:
+                finish(name, z["cross"][1])
+                finish(name, z["cross"][2])
+
+    for c in range(nc):
+        gives[c].wait()
 
 
 def line_call(query, cache, head_of_slot, lengths, out_weight, cuts):
@@ -725,7 +788,7 @@
         functools.partial(line_kernel, (tuple(parts), hl, ns, Lb, hd, G)),
         out_shape=jax.ShapeDtypeStruct((per_tp, T, columns), bf),
         in_specs=[smem, smem, anywhere, anywhere, anywhere],
-        out_specs=pl.BlockSpec(memory_space=pltpu.VMEM),
+        out_specs=anywhere,
         scratch_shapes=[
             v(cache.shape, bf),
             v((ns, B, Lb, 2 * hd), bf),
@@ -747,12 +810,14 @@
             [v((2, tt, columns), bf) for tt in sizes],
             [v((2, tt, columns), bf) for tt in sizes],
             dma((B,)), dma(()), dma((nc,)),
-            dma((nc, 5)), dma((nc, 5)),
-            dma((nc, n_seq)), dma((nc, n_seq)),
-            dma((nc, n_seq)), dma((nc, n_seq)), dma((nc, n_seq)), dma((nc, n_seq)),
-            dma((nc, 5)), dma((nc, 4)), dma((nc, 5)), dma((nc, 4)),
-            dma((nc, n_seq)), dma((nc, n_seq)),
-            dma((nc, 5)), dma((nc, 4)),
+            dma((SLOTS, 5)), dma((nc, 3)),
+            dma((SLOTS, n_seq - 1)), dma((nc, n_seq - 1)),
+            dma((SLOTS, n_seq - 1)), dma((nc, n_seq - 1)),
+            dma((SLOTS, n_seq - 1)), dma((nc, n_seq - 1)),
+            dma((SLOTS, 5)), dma((nc, 4)), dma((SLOTS, 5)), dma((nc, 4)),
+            dma((SLOTS, n_seq - 1)), dma((nc, n_seq - 1)),
+            dma((SLOTS, 5)), dma((nc, 4)),
+            v((per_tp, T, columns), bf), dma((nc,)),
         ],
         compiler_params=pltpu.CompilerParams(
             collective_id=2, has_side_effects=True, vmem_limit_bytes=60 * 2**20

time: 117 us -> 112 us (0.957)
  Pallas kernels: 115 us -> 110 us
    pallas_call x1, Pallas kernels: 115 us -> 110 us  [line_call(): pl.pallas_call(functools.partial(line_kernel, (tuple(parts), hl, ns, Lb,...]
where the time goes in v3:
time: 112 us
  Pallas kernels  110 us (98%)
  local copies, waits for them, and re-layouts  1.88 us (2%)
    pallas_call x1, Pallas kernels, line_call(): pl.pallas_call(functools.partial(line_kernel, (tuple(parts), hl, ns, Lb,...  110 us

profile of v3, /device:TPU:0, one launch (start us, length us, event | category | flops | bytes accessed | tf_op | source)
XLA Modules:
  0.0 111.8 jit_solution(10798375128622428181)
XLA Ops:
  0.0 109.9 %shard_map.55 = bf16[2,64,2048]{2,1,0:T(8,128)(2,1)} custom-call(s32[8]{0:T(128)} %hos.1, s32[8]{0:T(128)} %lens.1, bf16[8,64,2048]{2,1,0:T(8,128)(2,1)} %q_hbm.1, bf16[8,1024,2,256]{3,2,1,0:T(2,128)(2,1)} %kv_hbm.1, bf16[2048,2048]{1,0:T(8,128)(2,1)} %w_hbm.1), custom_call_target="tpu_custom_call" | custom-call | tf_op jit(solution)/shard_map/pallas_call | solution.py:787
  109.9 1.9 %copy.7 = bf16[2,64,2048]{2,1,0:T(8,128)(2,1)} copy(bf16[2,64,2048]{2,1,0:T(8,128)(2,1)} %shard_map.55) | data formatting | bytes 1048576
